TPU v7x, 256 devices: a whole 4x4x8 slice. The times are simulated.
256 devices in a mesh: dp: 16 (over x, y), mp: 16 (over z, core).
Axes of the slice: x: 4, y: 4, z: 8, core: 2. Of those that a mesh axis runs over, the one named last changes fastest.
Arguments:
- hidden_in: bfloat16 [2048, 4096], P('dp', 'mp'), may hold values from -6 to 6
- lengths: int32 [16], P('dp'), may hold values from 1 to 128
- norm_attn: float32 [4096], replicated, may hold values from 0.25 to 1.75
- q_weight: bfloat16 [4096, 4096], P('dp', 'mp'), may hold values from -0.01171875 to 0.01171875
- k_weight: bfloat16 [4096, 4096], P('dp', 'mp'), may hold values from -0.09375 to 0.09375
- v_weight: bfloat16 [4096, 4096], P('dp', 'mp'), may hold values from -0.09375 to 0.09375
- out_weight_t: bfloat16 [4096, 4096], P('dp', 'mp'), may hold values from -0.09375 to 0.09375
- norm_ffn: float32 [4096], replicated, may hold values from 0.25 to 1.75
- gate_weight: bfloat16 [4096, 10240], P('dp', 'mp'), may hold values from -0.09375 to 0.09375
- up_weight: bfloat16 [4096, 10240], P('dp', 'mp'), may hold values from -0.09375 to 0.09375
- down_weight_t: bfloat16 [4096, 10240], P('dp', 'mp'), may hold values from -0.0625 to 0.0625
- scale_key: float32 [4096], P('mp'), may hold values from 0.25 to 4
- scale_value: float32 [4096], P('mp'), may hold values from 0.1 to 1.9
- scale_ffn: float32 [10240], P('mp'), may hold values from 0.1 to 1.9
- out_grad: bfloat16 [2048, 4096], P('dp'), may hold values from -6 to 6
- position_bias: float32 [64, 128, 128], P('mp'), may hold values from -6 to 256
Outputs:
- block_out: bfloat16 [2048, 4096], P('dp', 'mp')
- input_grad: bfloat16 [2048, 4096], P('dp', 'mp')
- grad_key: float32 [4096], P('mp')
- grad_value: float32 [4096], P('mp')
- grad_ffn: float32 [10240], P('mp')
Inputs may be any that keep to these rules, and one draw needn't show every extreme that they name: Keys of sequence b at positions lengths[b] and beyond are padding.
All inputs are finite; a program needn't handle non-finite values.
Results may differ from a plain program's by a relative error of at most 0.03.
Values may be sent and summed in bfloat16 or wider, within the bound.
A program may use at most 128 MiB of HBM per device.

v0:
```python
import functools
import jax
import jax.numpy as jnp
from jax import lax
from jax.sharding import Mesh
from jax.sharding import PartitionSpec as P

HEAD_DIM = 64
MP = ("mp_0", "mp_1")
DP = ("dp_0", "dp_1")
EPSILON = 1e-06
NEGATIVE = -1e30


def side_by_side(arrays, axis, dim, along):
    ends, at = ([], 0)
    for a in arrays[:-1]:
        at += a.shape[along]
        ends.append(at)
    both = jnp.concatenate(arrays, axis=along)
    return tuple(jnp.split(lax.all_gather(both, axis, axis=dim, tiled=True), ends, axis=along))


def in_blocks(x, dim, devices):
    dims = x.shape
    blocks = x.reshape(*dims[:dim], devices, dims[dim] // devices, *dims[dim + 1 :])
    return jnp.moveaxis(blocks, dim, 0)


def summed_on_arrival(x, axis, dim):
    blocks = in_blocks(x, dim, lax.axis_size(axis))
    arrived = lax.all_to_all(blocks, axis, split_axis=0, concat_axis=0, tiled=True)
    return arrived.astype(jnp.float32).sum(axis=0)


def summed_rows(x, axes, dim):
    far, near = axes
    blocks = in_blocks(x, dim, lax.axis_size(far))
    nearer = summed_on_arrival(blocks, near, dim + 1)
    arrived = lax.all_to_all(
        nearer.astype(jnp.bfloat16), far, split_axis=0, concat_axis=0, tiled=True
    )
    return arrived.astype(jnp.float32).sum(axis=0)


def filled_up(lines, devices):
    spare = -len(lines) % devices
    return jnp.pad(lines, [(0, spare)] + [(0, 0)] * (lines.ndim - 1))


def from_everyone(x, axis):
    copies = jnp.broadcast_to(x, (lax.axis_size(axis), *x.shape))
    return lax.all_to_all(copies, axis, split_axis=0, concat_axis=0, tiled=True)


def laid_out(blocks, dim):
    dims = list(blocks.shape[1:])
    dims[dim] *= blocks.shape[0]
    return jnp.moveaxis(blocks, 0, dim).reshape(dims)


def gather_axes(x, axes, dim):
    far, near = axes
    blocks = from_everyone(from_everyone(x, far), near)
    return laid_out(blocks.swapaxes(0, 1).reshape(-1, *x.shape), dim)


def sum_by_parts(x, axes):
    lines = x.reshape(-1, x.shape[-1])
    own = summed_rows(filled_up(lines, lax.axis_size(axes[0]) * lax.axis_size(axes[1])), axes, 0)
    whole = gather_axes(own.astype(jnp.bfloat16), axes, 0)
    return whole[: len(lines)].reshape(x.shape).astype(jnp.float32)


def of_everyone(x, axis):
    everything = from_everyone(x, axis)
    return jnp.sum(everything, axis=0)


def over_axes(x, axes):
    return functools.reduce(lax.psum, axes, x)


def inverse_rms(values):
    return lax.rsqrt(jnp.mean(values * values, axis=-1, keepdims=True) + EPSILON)


def gelu_tanh(values):
    return jax.nn.gelu(values, approximate=True)


def contract_last(left_side, right_side):
    return lax.dot_general(
        left_side, right_side, (((1,), (1,)), ((), ())), preferred_element_type=jnp.float32
    )


def norm_back(grad_in, values, inverse, gain_vec):
    scaled = grad_in * gain_vec
    correction = (
        values * inverse * inverse * inverse * jnp.mean(scaled * values, axis=-1, keepdims=True)
    )
    return inverse * scaled - correction


def on_device(
    hidden_in,
    lengths,
    norm_attn,
    q_weight,
    k_weight,
    v_weight,
    out_weight_t,
    norm_ffn,
    gate_weight,
    up_weight,
    down_weight_t,
    scale_key,
    scale_value,
    scale_ffn,
    out_grad,
    position_bias,
):
    full_inputs = lax.all_gather(hidden_in, MP, axis=1, tiled=True)
    q_full, k_full, v_full, o_full, gate_full, up_full, down_full = side_by_side(
        (q_weight, k_weight, v_weight, out_weight_t, gate_weight, up_weight, down_weight_t),
        DP,
        0,
        1,
    )
    seq_local = lengths.shape[0]
    tokens_local = full_inputs.shape[0]
    seq_len = tokens_local // seq_local
    heads_local = q_full.shape[1] // HEAD_DIM
    shaped = (seq_local, seq_len, heads_local, HEAD_DIM)
    inputs32 = full_inputs.astype(jnp.float32)
    inv_first = inverse_rms(inputs32)
    normed_first = (inputs32 * inv_first * norm_attn).astype(jnp.bfloat16)
    queries = jnp.dot(normed_first, q_full, preferred_element_type=jnp.float32).astype(jnp.bfloat16)
    key_pre = jnp.dot(normed_first, k_full, preferred_element_type=jnp.float32)
    value_pre = jnp.dot(normed_first, v_full, preferred_element_type=jnp.float32)
    key_rows = (key_pre * scale_key).astype(jnp.bfloat16)
    value_rows = (value_pre * scale_value).astype(jnp.bfloat16)
    q_heads = queries.reshape(shaped)
    k_heads = key_rows.reshape(shaped)
    v_heads = value_rows.reshape(shaped)
    scores = (
        jnp.einsum("bihe,bjhe->bhij", q_heads, k_heads, preferred_element_type=jnp.float32)
        + position_bias[None]
    )
    positions = lax.broadcasted_iota(jnp.int32, (seq_local, seq_len), 1)
    valid_keys = positions < lengths[:, None]
    scores = jnp.where(valid_keys[:, None, None, :], scores, NEGATIVE)
    largest = jnp.max(scores, axis=-1, keepdims=True)
    exponent = jnp.exp(scores - largest)
    attn_probs = exponent / jnp.sum(exponent, axis=-1, keepdims=True)
    probs_low = attn_probs.astype(jnp.bfloat16)
    context = (
        jnp.einsum("bhij,bjhe->bihe", probs_low, v_heads, preferred_element_type=jnp.float32)
        .reshape(tokens_local, -1)
        .astype(jnp.bfloat16)
    )
    attended = sum_by_parts(contract_last(context, o_full).astype(jnp.bfloat16), ("mp_0", "mp_1"))
    first_sum = inputs32 + attended
    inv_second = inverse_rms(first_sum)
    normed_second = (first_sum * inv_second * norm_ffn).astype(jnp.bfloat16)
    gate_proj = jnp.dot(normed_second, gate_full, preferred_element_type=jnp.float32)
    upward = jnp.dot(normed_second, up_full, preferred_element_type=jnp.float32)
    activated, gelu_back = jax.vjp(gelu_tanh, gate_proj)
    product = activated * upward
    hidden = (product * scale_ffn).astype(jnp.bfloat16)
    ffn_share = summed_on_arrival(contract_last(hidden, down_full).astype(jnp.bfloat16), MP, 1)
    share_width = ffn_share.shape[1]
    offset = lax.axis_index(MP) * share_width
    first_share = lax.dynamic_slice_in_dim(first_sum, offset, share_width, 1)
    block_out = (first_share + ffn_share).astype(jnp.bfloat16)
    d_hidden = jnp.dot(out_grad, down_full, preferred_element_type=jnp.float32)
    grad_ffn_part = jnp.sum(d_hidden * product, axis=0)
    d_product = d_hidden * scale_ffn
    d_gate = gelu_back(d_product * upward)[0].astype(jnp.bfloat16)
    d_up = (d_product * activated).astype(jnp.bfloat16)
    d_second = sum_by_parts(
        (contract_last(d_gate, gate_full) + contract_last(d_up, up_full)).astype(jnp.bfloat16),
        ("mp_0", "mp_1"),
    )
    d_first = out_grad.astype(jnp.float32) + norm_back(d_second, first_sum, inv_second, norm_ffn)
    d_context = jnp.dot(
        d_first.astype(jnp.bfloat16), o_full, preferred_element_type=jnp.float32
    ).astype(jnp.bfloat16)
    dc_heads = d_context.reshape(shaped)
    d_probs = jnp.einsum("bihe,bjhe->bhij", dc_heads, v_heads, preferred_element_type=jnp.float32)
    d_scores = (
        attn_probs * (d_probs - jnp.sum(attn_probs * d_probs, axis=-1, keepdims=True))
    ).astype(jnp.bfloat16)
    d_values = jnp.einsum(
        "bhij,bihe->bjhe", probs_low, dc_heads, preferred_element_type=jnp.float32
    ).reshape(tokens_local, -1)
    d_keys = jnp.einsum(
        "bhij,bihe->bjhe", d_scores, q_heads, preferred_element_type=jnp.float32
    ).reshape(tokens_local, -1)
    d_queries = (
        jnp.einsum("bhij,bjhe->bihe", d_scores, k_heads, preferred_element_type=jnp.float32)
        .reshape(tokens_local, -1)
        .astype(jnp.bfloat16)
    )
    grad_key_part = jnp.sum(d_keys * key_pre, axis=0)
    grad_value_part = jnp.sum(d_values * value_pre, axis=0)
    d_key_pre = (d_keys * scale_key).astype(jnp.bfloat16)
    d_value_pre = (d_values * scale_value).astype(jnp.bfloat16)
    attn_term = (
        contract_last(d_queries, q_full)
        + contract_last(d_key_pre, k_full)
        + contract_last(d_value_pre, v_full)
    )
    d_share = summed_on_arrival(attn_term.astype(jnp.bfloat16), MP, 1)
    gain_share = lax.dynamic_slice_in_dim(norm_attn, offset, share_width, 0)
    input_share = lax.dynamic_slice_in_dim(inputs32, offset, share_width, 1)
    first_grad_share = lax.dynamic_slice_in_dim(d_first, offset, share_width, 1)
    scaled_grad = d_share * gain_share
    dot_share = jnp.sum(scaled_grad * input_share, axis=-1, keepdims=True)
    dot_total = of_everyone(dot_share, MP)
    mean_dot = dot_total / inputs32.shape[1]
    cubed = inv_first * inv_first * inv_first
    input_grad = (
        first_grad_share + inv_first * scaled_grad - input_share * cubed * mean_dot
    ).astype(jnp.bfloat16)
    grad_key, grad_value, grad_ffn = (
        over_axes(grad_key_part, DP),
        over_axes(grad_value_part, DP),
        over_axes(grad_ffn_part, DP),
    )
    return (block_out, input_grad, grad_key, grad_value, grad_ffn)


def solution(mesh):
    finer = Mesh(mesh.devices.reshape(4, 4, 8, 2), ("dp_0", "dp_1", "mp_0", "mp_1"))
    placed = (
        P(DP, MP),
        P(DP),
        P(),
        P(DP, MP),
        P(DP, MP),
        P(DP, MP),
        P(DP, MP),
        P(),
        P(DP, MP),
        P(DP, MP),
        P(DP, MP),
        P(MP),
        P(MP),
        P(MP),
        P(DP, None),
        P(MP, None, None),
    )
    return jax.shard_map(
        on_device,
        mesh=finer,
        in_specs=placed,
        out_specs=(P(DP, MP), P(DP, MP), P(MP), P(MP), P(MP)),
        check_vma=False,
    )
```

profile of v0, /device:TPU:1, one launch (start us, length us, event | category | flops | bytes accessed | tf_op | source)
XLA Modules:
  0.0 437.9 jit_solution(16360203652515288852)
XLA Ops:
  7.2 0.7 all-gather.3.cloned.1.call-update
  8.0 0.9 constant_dynamic-update-slice_fusion.6
  8.9 1.0 constant_dynamic-update-slice_fusion.5
  9.8 0.9 constant_dynamic-update-slice_fusion.4
  10.8 0.9 constant_dynamic-update-slice_fusion.3
  11.7 1.0 constant_dynamic-update-slice_fusion.2
  12.7 1.0 constant_dynamic-update-slice_fusion.1
  13.8 1.2 copy-done.3
  15.9 35.3 %all-gather.3.cloned.1.call-done = bf16[128,4096]{1,0:T(8,128)(2,1)} async-done(((bf16[128,256]{1,0:T(8,128)(2,1)}), bf16[128,4096]{1,0:T(8,128)(2,1)}) %all-gather.3.cloned.1.call-update) | async-done | bytes 1048592 | tf_op jit(solution)/shard_map/all_gather | solution.py:124
  51.2 1.5 multiply_reduce_fusion.2
  53.2 152.8 %all-gather.5.cloned.1.call-done = bf16[4096,2944]{1,0:T(8,128)(2,1)} async-done(((bf16[256,2944]{1,0:T(8,128)(2,1)}), bf16[4096,2944]{1,0:T(8,128)(2,1)}) %all-gather.5.cloned.1.call-update) | async-done | bytes 24117264 | tf_op jit(solution)/shard_map/all_gather | solution.py:21
  206.1 3.1 multiply_convert_fusion.10
  209.4 2.1 fusion.32
  211.6 2.7 multiply_convert_fusion.9
  215.4 2.4 convolution_convert_fusion.1
  218.0 5.0 %all_to_all.55 = bf16[2,8,8,4096]{3,2,1,0:T(8,128)(2,1)S(1)} all-to-all(bf16[2,8,8,4096]{3,2,1,0:T(8,128)(2,1)S(1)} %bitcast.82), channel_id=1, replica_groups=mesh['dp_0'=4,'dp_1'=4,'mp_0'=8,'mp_1'=2] {'mp_1'}, dimensions={0} | all-to-all | bytes 2097152 | tf_op jit(solution)/shard_map/all_to_all | solution.py:32
  223.4 23.3 %all_to_all.56 = bf16[8,8,4096]{2,1,0:T(8,128)(2,1)S(1)} all-to-all(bf16[8,8,4096]{2,1,0:T(8,128)(2,1)S(1)} %reduce_sum.158), channel_id=1, replica_groups=mesh['dp_0'=4,'dp_1'=4,'mp_0'=8,'mp_1'=2] {'mp_0'}, dimensions={0} | all-to-all | bytes 1048576 | tf_op jit(solution)/shard_map/all_to_all | solution.py:40
  246.8 17.5 %all_to_all.57 = bf16[8,8,4096]{2,1,0:T(8,128)(2,1)S(1)} all-to-all(bf16[8,8,4096]{2,1,0:T(8,128)(2,1)S(1)} %broadcast_in_dim.24), channel_id=1, replica_groups=mesh['dp_0'=4,'dp_1'=4,'mp_0'=8,'mp_1'=2] {'mp_0'}, dimensions={0} | all-to-all | bytes 1048576 | tf_op jit(solution)/shard_map/all_to_all | solution.py:53
  264.4 7.5 %all_to_all.58 = bf16[2,8,8,4096]{3,2,1,0:T(8,128)(2,1)S(1)} all-to-all(bf16[2,8,8,4096]{3,2,1,0:T(8,128)(2,1)S(1)} %broadcast_in_dim.25), channel_id=1, replica_groups=mesh['dp_0'=4,'dp_1'=4,'mp_0'=8,'mp_1'=2] {'mp_1'}, dimensions={0} | all-to-all | bytes 2097152 | tf_op jit(solution)/shard_map/all_to_all | solution.py:53
  272.9 3.5 fusion.7
  276.4 3.7 fusion.11
  280.1 3.7 multiply_reduce_fusion.3
  283.8 4.3 fusion.9
  288.2 4.3 fusion.1
  292.5 5.4 %all_to_all.59 = bf16[2,8,8,4096]{3,2,1,0:T(8,128)(2,1)} all-to-all(bf16[2,8,8,4096]{3,2,1,0:T(8,128)(2,1)S(1)} %bitcast.83), channel_id=1, replica_groups=mesh['dp_0'=4,'dp_1'=4,'mp_0'=8,'mp_1'=2] {'mp_1'}, dimensions={0} | all-to-all | bytes 2097152 | tf_op jit(solution)/shard_map/all_to_all | solution.py:32
  297.9 2.4 reduce_sum.162
  300.3 22.1 %all_to_all.60 = bf16[8,8,4096]{2,1,0:T(8,128)(2,1)} all-to-all(bf16[8,8,4096]{2,1,0:T(8,128)(2,1)} %reduce_sum.162), channel_id=1, replica_groups=mesh['dp_0'=4,'dp_1'=4,'mp_0'=8,'mp_1'=2] {'mp_0'}, dimensions={0} | all-to-all | bytes 1048576 | tf_op jit(solution)/shard_map/all_to_all | solution.py:40
  322.4 1.1 reduce_sum.163
  323.5 0.8 broadcast_in_dim.26
  324.3 4.3 all-to-all-start.7
  328.7 4.5 %convolution_convert_fusion = bf16[128,4096]{1,0:T(8,128)(2,1)S(1)} fusion(bf16[4096,2944]{1,0:T(8,128)(2,1)} %all-gather.5.cloned.1.call-done, f32[640]{0:T(1024)S(1)} %copy-done.17, f32[128,640]{1,0:T(8,128)} %copy-done.24, f32[128,640]{1,0:T(8,128)} %copy-done.9), kind=kOutput, calls=%fused_computation.6 | convolution fusion | flops 672514048 | bytes 6949376 | tf_op jit(solution)/shard_map/dot_general | solution.py:93
  333.1 1.1 copy.118
  334.2 10.9 %all-to-all-done.7 = bf16[8,8,4096]{2,1,0:T(8,128)(2,1)} async-done(((bf16[8,8,4096]{2,1,0:T(8,128)(2,1)}), bf16[8,8,4096]{2,1,0:T(8,128)(2,1)}, u32[]{:S(2)}, u32[]{:S(2)}) %all-to-all-start.7) | async-done | bytes 524320 | tf_op jit(solution)/shard_map/all_to_all | solution.py:53
  345.1 1.1 broadcast_in_dim.27
  346.3 5.5 %all_to_all.61 = bf16[2,8,8,4096]{3,2,1,0:T(8,128)(2,1)} all-to-all(bf16[2,8,8,4096]{3,2,1,0:T(8,128)(2,1)S(1)} %broadcast_in_dim.27), channel_id=1, replica_groups=mesh['dp_0'=4,'dp_1'=4,'mp_0'=8,'mp_1'=2] {'mp_1'}, dimensions={0} | all-to-all | bytes 2097152 | tf_op jit(solution)/shard_map/all_to_all | solution.py:53
  351.8 4.4 %all-to-all-start.4 = ((bf16[16,128,256]{2,1,0:T(8,128)(2,1)}), bf16[16,128,256]{2,1,0:T(8,128)(2,1)}, u32[]{:S(2)}, u32[]{:S(2)}) async-start(bf16[16,128,256]{2,1,0:T(8,128)(2,1)} %bitcast.81), calls=%async_computation.4 | async-start | bytes 2097152 | tf_op jit(solution)/shard_map/all_to_all | solution.py:32
  356.2 1.7 multiply_reduce_fusion
  358.1 0.7 subtract_add_fusion
  358.8 1.4 copy-done.2
  360.2 2.1 fusion.35
  362.3 0.7 copy.95
  363.1 1.1 multiply_reduce_fusion.4
  364.2 1.0 fusion.74
  365.4 1.9 fusion.57
  367.3 1.0 copy.100
  368.3 1.0 convolution_convert_fusion.2
  369.3 2.4 fusion.19
  371.7 2.4 convolution_add_fusion.1
  374.1 2.5 fusion.2
  376.6 1.1 copy.117
  377.7 6.7 %all-to-all-done.4 = bf16[16,128,256]{2,1,0:T(8,128)(2,1)} async-done(((bf16[16,128,256]{2,1,0:T(8,128)(2,1)}), bf16[16,128,256]{2,1,0:T(8,128)(2,1)}, u32[]{:S(2)}, u32[]{:S(2)}) %all-to-all-start.4) | async-done | bytes 1048608 | tf_op jit(solution)/shard_map/all_to_all | solution.py:32
  384.4 4.2 all-to-all-start.9
  388.6 0.8 dynamic_slice.14
  389.4 1.6 convert_element_type.124
  391.1 9.3 %all-reduce.1 = (f32[256]{0:T(256)S(1)}, f32[256]{0:T(256)S(1)}, f32[640]{0:T(1024)S(1)}) all-reduce(f32[256]{0:T(256)S(1)} %get-tuple-element.26, f32[256]{0:T(256)S(1)} %get-tuple-element.25, f32[640]{0:T(1024)S(1)} %get-tuple-element.23), channel_id=1, replica_groups=mesh['dp_0'=4,'dp_1'=4,'mp_0'=8,'mp_1'=2] {'dp_0'}, use_global_device_ids=true, to_apply=%region_15.16 | all-reduce | flops 1152 | bytes 9216 | tf_op jit(solution)/shard_map/psum | solution.py:81
  400.4 8.0 %all-reduce = (f32[256]{0:T(256)}, f32[256]{0:T(256)}, f32[640]{0:T(1024)}) all-reduce(f32[256]{0:T(256)S(1)} %get-tuple-element.8, f32[256]{0:T(256)S(1)} %get-tuple-element.9, f32[640]{0:T(1024)S(1)} %get-tuple-element.10), channel_id=1, replica_groups=mesh['dp_0'=4,'dp_1'=4,'mp_0'=8,'mp_1'=2] {'dp_1'}, use_global_device_ids=true, to_apply=%region_16.17 | all-reduce | flops 1152 | bytes 9216 | tf_op jit(solution)/shard_map/psum | solution.py:81
  408.4 1.4 convert_reduce_fusion.1
  409.8 6.0 %all-to-all-done.9 = bf16[16,128,256]{2,1,0:T(8,128)(2,1)} async-done(((bf16[16,128,256]{2,1,0:T(8,128)(2,1)}), bf16[16,128,256]{2,1,0:T(8,128)(2,1)}, u32[]{:S(2)}, u32[]{:S(2)}) %all-to-all-start.9) | async-done | bytes 1048608 | tf_op jit(solution)/shard_map/all_to_all | solution.py:32
  415.8 1.4 convert_reduce_fusion
  417.2 1.0 multiply_reduce_fusion.7
  418.8 3.5 all-to-all-start.10
  422.3 0.7 add_convert_fusion
  423.0 6.3 %all-to-all-done.10 = f32[16,128,1]{1,2,0:T(1,128)S(1)} async-done(((f32[16,128,1]{1,2,0:T(1,128)}), f32[16,128,1]{1,2,0:T(1,128)S(1)}, u32[]{:S(2)}, u32[]{:S(2)}) %all-to-all-start.10) | async-done | bytes 8224 | tf_op jit(solution)/shard_map/all_to_all | solution.py:53
  429.4 1.7 subtract_convert_fusion
  (77 shorter events, 4.7 us)
Async XLA Ops:
  7.2 6.6 %copy-start.10 = (bf16[256,640]{1,0:T(8,128)(2,1)S(1)}, bf16[256,640]{1,0:T(8,128)(2,1)}, u32[]{:S(2)}) copy-start(bf16[256,640]{1,0:T(8,128)(2,1)} %param.26) | copy-start | bytes 983044
  7.2 44.0 %all-gather.3.cloned.1.call-start = ((), (), s32[]{:S(2)}) async-start(), calls=%async_computation.11 | async-start | bytes 1114112 | tf_op jit(solution)/shard_map/all_gather | solution.py:124
  7.9 198.2 %all-gather.5.cloned.1.call-start = ((), (), s32[]{:S(2)}) async-start(), calls=%async_computation.12 | async-start | bytes 25624576 | tf_op jit(solution)/shard_map/all_gather | solution.py:21
  8.9 6.2 %copy-start.11 = (f32[4,128,128]{2,1,0:T(8,128)S(1)}, f32[4,128,128]{2,1,0:T(8,128)}, u32[]{:S(2)}) copy-start(f32[4,128,128]{2,1,0:T(8,128)} %param.31) | copy-start | bytes 786436
  12.7 193.4 %copy-start.18 = (f32[256]{0:T(256)S(1)}, f32[256]{0:T(256)}, u32[]{:S(2)}) copy-start(f32[256]{0:T(256)} %param.28) | copy-start | bytes 3076
  12.7 193.4 %copy-start.23 = (f32[4096]{0:T(1024)S(1)}, f32[4096]{0:T(1024)}, u32[]{:S(2)}) copy-start(f32[4096]{0:T(1024)} %param.18) | copy-start | bytes 49156
  13.8 1.2 copy-start.3
  53.2 158.4 %copy-start.21 = (f32[128]{0:T(128)}, f32[128]{0:T(128)S(1)}, u32[]{:S(2)}) copy-start(f32[128]{0:T(128)S(1)} %get-tuple-element.14) | copy-start | bytes 1540
  206.1 3.2 copy-start
  209.3 5.7 %copy-start.15 = (bf16[128,256]{0,1:T(8,128)(2,1)}, bf16[128,256]{0,1:T(8,128)(2,1)S(1)}, u32[]{:S(2)}) copy-start(bf16[128,256]{0,1:T(8,128)(2,1)S(1)} %copy.85) | copy-start | bytes 196612
  209.3 2.3 copy-start.19
  211.6 2.9 copy-start.7
  214.5 0.8 copy-start.8
  214.7 0.7 copy-start.4
  272.1 0.7 copy-start.14
  276.4 7.4 %copy-start.24 = (f32[128,640]{1,0:T(8,128)}, f32[128,640]{1,0:T(8,128)S(1)}, u32[]{:S(2)}) copy-start(f32[128,640]{1,0:T(8,128)S(1)} %fusion.7) | copy-start | bytes 983044
  276.4 3.7 copy-start.5
  280.1 8.0 %copy-start.9 = (f32[128,640]{1,0:T(8,128)}, f32[128,640]{1,0:T(8,128)S(1)}, u32[]{:S(2)}) copy-start(f32[128,640]{1,0:T(8,128)S(1)} %fusion.11) | copy-start | bytes 983044
  280.1 3.7 copy-start.17
  324.3 20.8 %all-to-all-start.7 = ((bf16[8,8,4096]{2,1,0:T(8,128)(2,1)}), bf16[8,8,4096]{2,1,0:T(8,128)(2,1)}, u32[]{:S(2)}, u32[]{:S(2)}) async-start(bf16[8,8,4096]{2,1,0:T(8,128)(2,1)} %broadcast_in_dim.26), calls=%async_computation.7 | async-start | bytes 1048576 | tf_op jit(solution)/shard_map/all_to_all | solution.py:53
  351.8 32.6 %all-to-all-start.4 = ((bf16[16,128,256]{2,1,0:T(8,128)(2,1)}), bf16[16,128,256]{2,1,0:T(8,128)(2,1)}, u32[]{:S(2)}, u32[]{:S(2)}) async-start(bf16[16,128,256]{2,1,0:T(8,128)(2,1)} %bitcast.81), calls=%async_computation.4 | async-start | bytes 2097152 | tf_op jit(solution)/shard_map/all_to_all | solution.py:32
  356.2 1.8 copy-start.1
  356.2 1.9 copy-start.6
  358.8 1.4 copy-start.2
  360.2 2.8 copy-start.16
  384.4 31.5 %all-to-all-start.9 = ((bf16[16,128,256]{2,1,0:T(8,128)(2,1)}), bf16[16,128,256]{2,1,0:T(8,128)(2,1)}, u32[]{:S(2)}, u32[]{:S(2)}) async-start(bf16[16,128,256]{2,1,0:T(8,128)(2,1)} %bitcast.80), calls=%async_computation.9 | async-start | bytes 2097152 | tf_op jit(solution)/shard_map/all_to_all | solution.py:32
  388.6 2.4 copy-start.12
  388.6 2.4 copy-start.13
  391.0 38.3 %copy-start.20 = (f32[128]{0:T(128)S(1)}, f32[128]{0:T(128)}, u32[]{:S(2)}) copy-start(f32[128]{0:T(128)} %get-tuple-element.13) | copy-start | bytes 1540
  391.0 38.3 %copy-start.22 = (f32[128]{0:T(128)S(1)}, f32[128]{0:T(128)}, u32[]{:S(2)}) copy-start(f32[128]{0:T(128)} %copy-done.21) | copy-start | bytes 1540
  418.8 10.5 %all-to-all-start.10 = ((f32[16,128,1]{1,2,0:T(1,128)}), f32[16,128,1]{1,2,0:T(1,128)S(1)}, u32[]{:S(2)}, u32[]{:S(2)}) async-start(f32[16,128,1]{1,2,0:T(1,128)} %broadcast_in_dim.28), calls=%async_computation.10 | async-start | bytes 16384 | tf_op jit(solution)/shard_map/all_to_all | solution.py:53
Sparse Core Ops, SparseCore 0:
  9.7 41.4 all-gather.2
  53.7 152.3 all-gather.4
where the time goes:
time: 440 us; the launch traced here: 438 us
  waiting for transfers between devices  219 us (50%)
  blocking collectives  104 us (24%)
  matrix products  49.2 us (11%)
  local copies, waits for them, and re-layouts  17.2 us (4%)
  other arithmetic  17.2 us (4%)
  starting transfers between devices  16.6 us (4%)
  between operations  15.3 us (3%)
    all_gather x1, waiting for transfers between devices, side_by_side(): lax.all_gather(both, axis, axis=dim, tiled=True)  153 us
    all_to_all x2, blocking collectives, summed_rows(): lax.all_to_all(nearer.astype(jnp.bfloat16), far, split_axis=0, concat_axi...  45.3 us
    all_gather x1, waiting for transfers between devices, on_device(): full_inputs = lax.all_gather(hidden_in, MP, axis=1, tiled=True)  35.3 us
    all_to_all x3, blocking collectives, from_everyone(): return lax.all_to_all(copies, axis, split_axis=0, concat_axis=0, tiled=True)  30.6 us
    dot_general x7, matrix products, contract_last(): lax.dot_general(left_side, right_side, (((1,), (1,)), ((), ())), preferre...  22.8 us
    psum x2, blocking collectives, over_axes(): return functools.reduce(lax.psum, axes, x)  17.3 us
    all_to_all x2, waiting for transfers between devices, from_everyone(): return lax.all_to_all(copies, axis, split_axis=0, concat_axis=0, tiled=True)  17.2 us
    all_to_all x2, waiting for transfers between devices, summed_on_arrival(): lax.all_to_all(blocks, axis, split_axis=0, concat_axis=0, tiled=True)  12.7 us
  transfers between devices with their start and end apart: 6, of which 6 were waited for; matrix products, arithmetic and copies ran while one was open for 9% of the time, Pallas kernels for 0%

commit v1 on v0

--- a/solution.py
+++ b/solution.py
@@ -121,7 +121,8 @@
     out_grad,
     position_bias,
 ):
-    full_inputs = lax.all_gather(hidden_in, MP, axis=1, tiled=True)
+    sent = jnp.stack([hidden_in] * lax.axis_size(MP))
+    full_inputs = jnp.concatenate(lax.all_to_all(sent, MP, 0, 0), axis=1)
     q_full, k_full, v_full, o_full, gate_full, up_full, down_full = side_by_side(
         (q_weight, k_weight, v_weight, out_weight_t, gate_weight, up_weight, down_weight_t),
         DP,

time: 440 us -> 418 us (0.950)
  waiting for transfers between devices: 219 us -> 183 us
  blocking collectives: 104 us -> 85.1 us
  local copies, waits for them, and re-layouts: 17.2 us -> 32.9 us
  starting transfers between devices: 16.6 us -> 29.7 us
  other arithmetic: 17.2 us -> 23.3 us
    all_gather x1, waiting for transfers between devices: 153 us -> 115 us  [side_by_side(): lax.all_gather(both, axis, axis=dim, tiled=True)]
    all_gather x1 -> x0, waiting for transfers between devices: 35.3 us -> none  [on_device(): full_inputs = lax.all_gather(hidden_in, MP, axis=1, tiled=True)]
    all_to_all x0 -> x1, waiting for transfers between devices: none -> 27.2 us  [on_device(): full_inputs = jnp.concatenate(lax.all_to_all(sent, MP, 0, 0), axis=1)]
    all_to_all x3 -> x2, blocking collectives: 30.6 us -> 12.3 us  [from_everyone(): return lax.all_to_all(copies, axis, split_axis=0, concat_axis=0, tiled=True)]
    convert_element_type x0 -> x4, local copies, waits for them, and re-layouts: none -> 10.8 us  [the longest x3 7.81 us: on_device(): inputs32 = full_inputs.astype(jnp.float32)]
    all_to_all x0 -> x1, starting transfers between devices: none -> 9.97 us  [on_device(): full_inputs = jnp.concatenate(lax.all_to_all(sent, MP, 0, 0), axis=1)]
    all_to_all x2 -> x3, waiting for transfers between devices: 17.2 us -> 24.7 us  [from_everyone(): return lax.all_to_all(copies, axis, split_axis=0, concat_axis=0, tiled=True)]
    all_to_all x2 -> x3, starting transfers between devices: 7.82 us -> 11.7 us  [from_everyone(): return lax.all_to_all(copies, axis, split_axis=0, concat_axis=0, tiled=True)]
  transfers between devices with their start and end apart: 6 -> 7, of which waited for: 6 -> 7; matrix products, arithmetic and copies ran while one was open for 9% -> 10% of each run, Pallas kernels for 0% -> 0%
where the time goes in v1:
time: 418 us; the launch traced here: 416 us
  waiting for transfers between devices  183 us (44%)
  blocking collectives  85.1 us (20%)
  matrix products  46.3 us (11%)
  local copies, waits for them, and re-layouts  32.9 us (8%)
  starting transfers between devices  29.7 us (7%)
  other arithmetic  23.3 us (6%)
  between operations  15.4 us (4%)
    all_gather x1, waiting for transfers between devices, side_by_side(): lax.all_gather(both, axis, axis=dim, tiled=True)  115 us
    all_to_all x2, blocking collectives, summed_rows(): lax.all_to_all(nearer.astype(jnp.bfloat16), far, split_axis=0, concat_axi...  45.3 us
    all_to_all x1, waiting for transfers between devices, on_device(): full_inputs = jnp.concatenate(lax.all_to_all(sent, MP, 0, 0), axis=1)  27.2 us
    all_to_all x3, waiting for transfers between devices, from_everyone(): return lax.all_to_all(copies, axis, split_axis=0, concat_axis=0, tiled=True)  24.7 us
    dot_general x7, matrix products, contract_last(): lax.dot_general(left_side, right_side, (((1,), (1,)), ((), ())), preferre...  22.6 us
    psum x2, blocking collectives, over_axes(): return functools.reduce(lax.psum, axes, x)  17.1 us
    all_to_all x2, waiting for transfers between devices, summed_on_arrival(): lax.all_to_all(blocks, axis, split_axis=0, concat_axis=0, tiled=True)  16.3 us
    all_to_all x2, blocking collectives, from_everyone(): return lax.all_to_all(copies, axis, split_axis=0, concat_axis=0, tiled=True)  12.3 us
  transfers between devices with their start and end apart: 7, of which 7 were waited for; matrix products, arithmetic and copies ran while one was open for 10% of the time, Pallas kernels for 0%

profile of v1, /device:TPU:1, one launch (start us, length us, event | category | flops | bytes accessed | tf_op | source)
XLA Modules:
  0.0 415.9 jit_solution(3819890919907943725)
XLA Ops:
  7.2 1.0 constant_dynamic-update-slice_fusion.6
  11.0 1.0 constant_dynamic-update-slice_fusion.2
  12.0 1.0 constant_dynamic-update-slice_fusion.1
  13.1 1.1 copy-done.5
  14.2 1.1 stack.2
  15.3 10.0 %all-to-all-start = ((bf16[16,128,256]{2,1,0:T(8,128)(2,1)}), bf16[16,128,256]{2,1,0:T(8,128)(2,1)S(1)}, u32[]{:S(2)}, u32[]{:S(2)}) async-start(bf16[16,128,256]{2,1,0:T(8,128)(2,1)} %stack.2), calls=%async_computation | async-start | bytes 2097152 | tf_op jit(solution)/shard_map/all_to_all | solution.py:125
  26.1 27.2 %all-to-all-done = bf16[16,128,256]{2,1,0:T(8,128)(2,1)S(1)} async-done(((bf16[16,128,256]{2,1,0:T(8,128)(2,1)}), bf16[16,128,256]{2,1,0:T(8,128)(2,1)S(1)}, u32[]{:S(2)}, u32[]{:S(2)}) %all-to-all-start) | async-done | bytes 1048608 | tf_op jit(solution)/shard_map/all_to_all | solution.py:125
  55.1 1.7 multiply_convert_fusion.1
  56.8 115.0 %all-gather.2.cloned.1.call-done = bf16[4096,2944]{1,0:T(8,128)(2,1)} async-done(((bf16[256,2944]{1,0:T(8,128)(2,1)}), bf16[4096,2944]{1,0:T(8,128)(2,1)}) %all-gather.2.cloned.1.call-update) | async-done | bytes 24117264 | tf_op jit(solution)/shard_map/all_gather | solution.py:21
  171.7 2.8 multiply_convert_fusion.9
  174.6 2.2 fusion.36
  177.5 2.8 multiply_convert_fusion.10
  180.6 2.4 convolution_convert_fusion.1
  183.1 5.0 %all_to_all.60 = bf16[2,8,8,4096]{3,2,1,0:T(8,128)(2,1)S(1)} all-to-all(bf16[2,8,8,4096]{3,2,1,0:T(8,128)(2,1)S(1)} %bitcast.108), channel_id=1, replica_groups=mesh['dp_0'=4,'dp_1'=4,'mp_0'=8,'mp_1'=2] {'mp_1'}, dimensions={0} | all-to-all | bytes 2097152 | tf_op jit(solution)/shard_map/all_to_all | solution.py:32
  188.6 23.3 %all_to_all.61 = bf16[8,8,4096]{2,1,0:T(8,128)(2,1)S(1)} all-to-all(bf16[8,8,4096]{2,1,0:T(8,128)(2,1)S(1)} %reduce_sum.158), channel_id=1, replica_groups=mesh['dp_0'=4,'dp_1'=4,'mp_0'=8,'mp_1'=2] {'mp_0'}, dimensions={0} | all-to-all | bytes 1048576 | tf_op jit(solution)/shard_map/all_to_all | solution.py:40
  212.7 4.1 all-to-all-start.3
  216.9 1.9 copy.125
  218.8 14.1 %all-to-all-done.3 = bf16[8,8,4096]{2,1,0:T(8,128)(2,1)} async-done(((bf16[8,8,4096]{2,1,0:T(8,128)(2,1)}), bf16[8,8,4096]{2,1,0:T(8,128)(2,1)}, u32[]{:S(2)}, u32[]{:S(2)}) %all-to-all-start.3) | async-done | bytes 524320 | tf_op jit(solution)/shard_map/all_to_all | solution.py:53
  232.9 1.1 broadcast_in_dim.25
  234.0 6.7 %all_to_all.62 = bf16[2,8,8,4096]{3,2,1,0:T(8,128)(2,1)S(1)} all-to-all(bf16[2,8,8,4096]{3,2,1,0:T(8,128)(2,1)S(1)} %broadcast_in_dim.25), channel_id=1, replica_groups=mesh['dp_0'=4,'dp_1'=4,'mp_0'=8,'mp_1'=2] {'mp_1'}, dimensions={0} | all-to-all | bytes 2097152 | tf_op jit(solution)/shard_map/all_to_all | solution.py:53
  240.7 1.0 copy-done
  241.9 1.7 bitcast_add_fusion
  243.6 2.0 copy.147
  245.6 3.0 copy.126
  248.6 2.3 multiply_reduce_fusion
  250.9 3.6 fusion.11
  254.6 3.8 fusion.7
  258.4 4.3 %multiply_reduce_fusion.2 = (f32[640]{0:T(1024)}, f32[128,640]{1,0:T(8,128)S(1)}) fusion(f32[128,640]{1,0:T(8,128)S(1)} %fusion.7, f32[128,640]{1,0:T(8,128)S(1)} %fusion.11, bf16[128,4096]{1,0:T(8,128)(2,1)S(1)} %copy-done.7, bf16[4096,2944]{1,0:T(8,128)(2,1)} %all-gather.2.cloned.1.call-done), kind=kOutput, calls=%fused_computation.71 | convolution fusion | flops 671989120 | bytes 7277056 | tf_op jit(solution)/shard_map/dot_general | solution.py:178
  262.6 4.3 %fusion.9 = f32[128,4096]{1,0:T(8,128)S(1)} fusion(bf16[4096,2944]{1,0:T(8,128)(2,1)} %all-gather.2.cloned.1.call-done, f32[128,640]{1,0:T(8,128)S(1)} %fusion.11, f32[128,640]{1,0:T(8,128)S(1)} %fusion.7, f32[128,640]{1,0:T(8,128)S(1)} %get-tuple-element.29, f32[640]{0:T(1024)S(1)} %copy-done.26), kind=kOutput, calls=%fused_computation.14 | convolution fusion | flops 672890880 | bytes 8325632 | tf_op jit(solution)/shard_map/dot_general | solution.py:93
  267.0 4.3 %fusion.1 = bf16[128,4096]{1,0:T(8,128)(2,1)S(1)} fusion(f32[128,4096]{1,0:T(8,128)S(1)} %fusion.9, bf16[4096,2944]{1,0:T(8,128)(2,1)} %all-gather.2.cloned.1.call-done, f32[128,640]{1,0:T(8,128)S(1)} %get-tuple-element.29, f32[640]{0:T(1024)S(1)} %copy-done.26, f32[128,640]{1,0:T(8,128)S(1)} %fusion.11), kind=kOutput, calls=%fused_computation.4 | convolution fusion | flops 673038336 | bytes 9046528 | tf_op jit(solution)/shard_map/dot_general | solution.py:93
  271.4 5.3 %all_to_all.63 = bf16[2,8,8,4096]{3,2,1,0:T(8,128)(2,1)} all-to-all(bf16[2,8,8,4096]{3,2,1,0:T(8,128)(2,1)S(1)} %bitcast.109), channel_id=1, replica_groups=mesh['dp_0'=4,'dp_1'=4,'mp_0'=8,'mp_1'=2] {'mp_1'}, dimensions={0} | all-to-all | bytes 2097152 | tf_op jit(solution)/shard_map/all_to_all | solution.py:32
  276.7 2.4 reduce_sum.162
  279.1 22.1 %all_to_all.64 = bf16[8,8,4096]{2,1,0:T(8,128)(2,1)} all-to-all(bf16[8,8,4096]{2,1,0:T(8,128)(2,1)} %reduce_sum.162), channel_id=1, replica_groups=mesh['dp_0'=4,'dp_1'=4,'mp_0'=8,'mp_1'=2] {'mp_0'}, dimensions={0} | all-to-all | bytes 1048576 | tf_op jit(solution)/shard_map/all_to_all | solution.py:40
  301.1 1.1 reduce_sum.163
  303.1 4.1 all-to-all-start.8
  307.2 1.5 convert_bitcast_fusion
  308.8 3.1 copy.130
  311.9 2.8 reshape.181
  314.7 4.3 %convolution_convert_fusion = bf16[128,4096]{1,0:T(8,128)(2,1)S(1)} fusion(bf16[4096,2944]{1,0:T(8,128)(2,1)} %all-gather.2.cloned.1.call-done, f32[640]{0:T(1024)S(1)} %copy-done.26, f32[128,640]{1,0:T(8,128)S(1)} %copy-done.35, f32[128,640]{1,0:T(8,128)S(1)} %copy-done.15), kind=kOutput, calls=%fused_computation.6 | convolution fusion | flops 672514048 | bytes 6949376 | tf_op jit(solution)/shard_map/dot_general | solution.py:93
  318.9 1.1 copy.159
  320.0 5.2 %all-to-all-done.8 = bf16[8,8,4096]{2,1,0:T(8,128)(2,1)} async-done(((bf16[8,8,4096]{2,1,0:T(8,128)(2,1)}), bf16[8,8,4096]{2,1,0:T(8,128)(2,1)}, u32[]{:S(2)}, u32[]{:S(2)}) %all-to-all-start.8) | async-done | bytes 524320 | tf_op jit(solution)/shard_map/all_to_all | solution.py:53
  325.2 1.1 broadcast_in_dim.27
  326.3 5.6 %all_to_all.65 = bf16[2,8,8,4096]{3,2,1,0:T(8,128)(2,1)} all-to-all(bf16[2,8,8,4096]{3,2,1,0:T(8,128)(2,1)S(1)} %broadcast_in_dim.27), channel_id=1, replica_groups=mesh['dp_0'=4,'dp_1'=4,'mp_0'=8,'mp_1'=2] {'mp_1'}, dimensions={0} | all-to-all | bytes 2097152 | tf_op jit(solution)/shard_map/all_to_all | solution.py:53
  332.0 4.5 %all-to-all-start.5 = ((bf16[16,128,256]{2,1,0:T(8,128)(2,1)}), bf16[16,128,256]{2,1,0:T(8,128)(2,1)}, u32[]{:S(2)}, u32[]{:S(2)}) async-start(bf16[16,128,256]{2,1,0:T(8,128)(2,1)} %bitcast.107), calls=%async_computation.5 | async-start | bytes 2097152 | tf_op jit(solution)/shard_map/all_to_all | solution.py:32
  336.5 2.4 fusion.16
  338.9 1.6 copy_convert_fusion
  341.8 1.3 copy-done.4
  343.1 2.1 fusion.39
  345.4 1.3 fusion.61
  347.6 2.4 fusion.23
  350.0 2.4 convolution_add_fusion.1
  352.5 2.4 fusion.2
  354.9 1.1 copy.158
  356.0 8.5 %all-to-all-done.5 = bf16[16,128,256]{2,1,0:T(8,128)(2,1)} async-done(((bf16[16,128,256]{2,1,0:T(8,128)(2,1)}), bf16[16,128,256]{2,1,0:T(8,128)(2,1)}, u32[]{:S(2)}, u32[]{:S(2)}) %all-to-all-start.5) | async-done | bytes 1048608 | tf_op jit(solution)/shard_map/all_to_all | solution.py:32
  364.6 3.6 all-to-all-start.10
  368.8 1.0 multiply_reduce_fusion.4
  369.7 9.2 %all-reduce.1 = (f32[256]{0:T(256)S(1)}, f32[256]{0:T(256)S(1)}, f32[640]{0:T(1024)S(1)}) all-reduce(f32[256]{0:T(256)S(1)} %get-tuple-element.31, f32[256]{0:T(256)S(1)} %get-tuple-element.30, f32[640]{0:T(1024)} %get-tuple-element.28), channel_id=1, replica_groups=mesh['dp_0'=4,'dp_1'=4,'mp_0'=8,'mp_1'=2] {'dp_0'}, use_global_device_ids=true, to_apply=%region_15.16 | all-reduce | flops 1152 | bytes 9216 | tf_op jit(solution)/shard_map/psum | solution.py:81
  379.0 7.9 %all-reduce = (f32[256]{0:T(256)}, f32[256]{0:T(256)}, f32[640]{0:T(1024)}) all-reduce(f32[256]{0:T(256)S(1)} %get-tuple-element.13, f32[256]{0:T(256)S(1)} %get-tuple-element.14, f32[640]{0:T(1024)S(1)} %get-tuple-element.15), channel_id=1, replica_groups=mesh['dp_0'=4,'dp_1'=4,'mp_0'=8,'mp_1'=2] {'dp_1'}, use_global_device_ids=true, to_apply=%region_16.17 | all-reduce | flops 1152 | bytes 9216 | tf_op jit(solution)/shard_map/psum | solution.py:81
  386.9 1.4 convert_reduce_fusion.1
  388.2 7.7 %all-to-all-done.10 = bf16[16,128,256]{2,1,0:T(8,128)(2,1)S(1)} async-done(((bf16[16,128,256]{2,1,0:T(8,128)(2,1)}), bf16[16,128,256]{2,1,0:T(8,128)(2,1)S(1)}, u32[]{:S(2)}, u32[]{:S(2)}) %all-to-all-start.10) | async-done | bytes 1048608 | tf_op jit(solution)/shard_map/all_to_all | solution.py:32
  396.9 3.4 all-to-all-start.11
  400.3 1.5 add_convert_fusion
  401.9 5.4 %all-to-all-done.11 = f32[16,128,1]{1,2,0:T(1,128)S(1)} async-done(((f32[16,128,1]{1,2,0:T(1,128)}), f32[16,128,1]{1,2,0:T(1,128)S(1)}, u32[]{:S(2)}, u32[]{:S(2)}) %all-to-all-start.11) | async-done | bytes 8224 | tf_op jit(solution)/shard_map/all_to_all | solution.py:53
  407.3 1.7 subtract_convert_fusion
  (110 shorter events, 12.3 us)
Async XLA Ops:
  7.2 5.8 %copy-start.16 = (bf16[256,640]{1,0:T(8,128)(2,1)S(1)}, bf16[256,640]{1,0:T(8,128)(2,1)}, u32[]{:S(2)}) copy-start(bf16[256,640]{1,0:T(8,128)(2,1)} %param.26) | copy-start | bytes 983044
  7.2 164.6 %all-gather.2.cloned.1.call-start = ((), (), s32[]{:S(2)}) async-start(), calls=%async_computation.12 | async-start | bytes 25624576 | tf_op jit(solution)/shard_map/all_gather | solution.py:21
  8.2 6.1 %copy-start.19 = (bf16[128,256]{1,0:T(8,128)(2,1)S(1)}, bf16[128,256]{1,0:T(8,128)(2,1)}, u32[]{:S(2)}) copy-start(bf16[128,256]{1,0:T(8,128)(2,1)} %param.16) | copy-start | bytes 196612
  13.1 1.1 copy-start.5
  13.1 12.2 %copy-start.17 = (f32[4,128,128]{2,1,0:T(8,128)S(1)}, f32[4,128,128]{2,1,0:T(8,128)}, u32[]{:S(2)}) copy-start(f32[4,128,128]{2,1,0:T(8,128)} %param.31) | copy-start | bytes 786436
  15.3 38.0 %all-to-all-start = ((bf16[16,128,256]{2,1,0:T(8,128)(2,1)}), bf16[16,128,256]{2,1,0:T(8,128)(2,1)S(1)}, u32[]{:S(2)}, u32[]{:S(2)}) async-start(bf16[16,128,256]{2,1,0:T(8,128)(2,1)} %stack.2), calls=%async_computation | async-start | bytes 2097152 | tf_op jit(solution)/shard_map/all_to_all | solution.py:125
  25.3 29.8 %copy-start.22 = (f32[4096]{0:T(1024)S(1)}, f32[4096]{0:T(1024)}, u32[]{:S(2)}) copy-start(f32[4096]{0:T(1024)} %param.18) | copy-start | bytes 49156
  55.1 1.7 copy-start.31
  55.1 116.7 %copy-start.29 = (f32[256]{0:T(256)S(1)}, f32[256]{0:T(256)}, u32[]{:S(2)}) copy-start(f32[256]{0:T(256)} %param.27) | copy-start | bytes 3076
  174.6 2.9 copy-start.11
  174.6 2.9 copy-start.27
  177.0 3.3 copy-start.9
  177.2 3.4 copy-start.6
  177.5 3.1 copy-start.24
  180.4 2.7 copy-start.20
  212.7 20.1 %all-to-all-start.3 = ((bf16[8,8,4096]{2,1,0:T(8,128)(2,1)}), bf16[8,8,4096]{2,1,0:T(8,128)(2,1)}, u32[]{:S(2)}, u32[]{:S(2)}) async-start(bf16[8,8,4096]{2,1,0:T(8,128)(2,1)} %broadcast_in_dim.24), calls=%async_computation.3 | async-start | bytes 1048576 | tf_op jit(solution)/shard_map/all_to_all | solution.py:53
  240.7 1.0 copy-start
  248.6 2.3 copy-start.2
  248.6 2.3 copy-start.18
  254.6 12.4 %copy-start.14 = (f32[128,640]{1,0:T(8,128)}, f32[128,640]{1,0:T(8,128)S(1)}, u32[]{:S(2)}) copy-start(f32[128,640]{1,0:T(8,128)S(1)} %fusion.11) | copy-start | bytes 983044
  254.6 3.8 copy-start.7
  258.4 4.3 %copy-start.34 = (f32[128,640]{1,0:T(8,128)}, f32[128,640]{1,0:T(8,128)S(1)}, u32[]{:S(2)}) copy-start(f32[128,640]{1,0:T(8,128)S(1)} %fusion.7) | copy-start | bytes 983044
  258.4 4.3 %copy-start.26 = (f32[640]{0:T(1024)S(1)}, f32[640]{0:T(1024)}, u32[]{:S(2)}) copy-start(f32[640]{0:T(1024)} %param.29) | copy-start | bytes 7684
  303.1 22.1 %all-to-all-start.8 = ((bf16[8,8,4096]{2,1,0:T(8,128)(2,1)}), bf16[8,8,4096]{2,1,0:T(8,128)(2,1)}, u32[]{:S(2)}, u32[]{:S(2)}) async-start(bf16[8,8,4096]{2,1,0:T(8,128)(2,1)} %broadcast_in_dim.26), calls=%async_computation.8 | async-start | bytes 1048576 | tf_op jit(solution)/shard_map/all_to_all | solution.py:53
  311.9 2.8 copy-start.15
  311.9 2.8 copy-start.35
  326.3 10.1 %copy-start.1 = (bf16[2,8,8,4096]{3,2,1,0:T(8,128)(2,1)S(1)}, bf16[2,8,8,4096]{3,2,1,0:T(8,128)(2,1)}, u32[]{:S(2)}) copy-start(bf16[2,8,8,4096]{3,2,1,0:T(8,128)(2,1)} %copy-done) | copy-start | bytes 3145732
  332.0 32.6 %all-to-all-start.5 = ((bf16[16,128,256]{2,1,0:T(8,128)(2,1)}), bf16[16,128,256]{2,1,0:T(8,128)(2,1)}, u32[]{:S(2)}, u32[]{:S(2)}) async-start(bf16[16,128,256]{2,1,0:T(8,128)(2,1)} %bitcast.107), calls=%async_computation.5 | async-start | bytes 2097152 | tf_op jit(solution)/shard_map/all_to_all | solution.py:32
  338.8 1.7 copy-start.8
  338.9 2.2 copy-start.3
  341.8 1.3 copy-start.4
  343.1 2.3 copy-start.25
  343.1 3.6 copy-start.21
  345.2 1.8 copy-start.10
  345.2 2.1 copy-start.12
  347.5 2.5 copy-start.30
  350.0 2.5 copy-start.28
  354.9 13.9 %copy-start.13 = (f32[128,256]{1,0:T(8,128)S(1)}, f32[128,256]{1,0:T(8,128)}, u32[]{:S(2)}) copy-start(f32[128,256]{1,0:T(8,128)} %get-tuple-element.23) | copy-start | bytes 393220
  364.6 31.4 %all-to-all-start.10 = ((bf16[16,128,256]{2,1,0:T(8,128)(2,1)}), bf16[16,128,256]{2,1,0:T(8,128)(2,1)S(1)}, u32[]{:S(2)}, u32[]{:S(2)}) async-start(bf16[16,128,256]{2,1,0:T(8,128)(2,1)} %bitcast.97), calls=%async_computation.10 | async-start | bytes 2097152 | tf_op jit(solution)/shard_map/all_to_all | solution.py:32
  368.8 27.4 %copy-start.23 = (f32[256]{0:T(256)S(1)}, f32[256]{0:T(256)}, u32[]{:S(2)}) copy-start(f32[256]{0:T(256)} %dynamic_slice.14) | copy-start | bytes 3076
  368.8 38.6 %copy-start.32 = (f32[128]{0:T(128)S(1)}, f32[128]{0:T(128)}, u32[]{:S(2)}) copy-start(f32[128]{0:T(128)} %copy-done.31) | copy-start | bytes 1540
  369.7 37.6 %copy-start.33 = (f32[128]{0:T(128)S(1)}, f32[128]{0:T(128)}, u32[]{:S(2)}) copy-start(f32[128]{0:T(128)} %get-tuple-element.18) | copy-start | bytes 1540
  396.9 10.4 %all-to-all-start.11 = ((f32[16,128,1]{1,2,0:T(1,128)}), f32[16,128,1]{1,2,0:T(1,128)S(1)}, u32[]{:S(2)}, u32[]{:S(2)}) async-start(f32[16,128,1]{1,2,0:T(1,128)} %broadcast_in_dim.28), calls=%async_computation.11 | async-start | bytes 16384 | tf_op jit(solution)/shard_map/all_to_all | solution.py:53
Sparse Core Ops, SparseCore 0:
  14.3 157.3 all-gather.1
